TPU v7x, 8 devices: a whole 2x2x1 slice. The times are simulated.
8 devices in a mesh: fsdp: 8 (over z, y, x, core).
Axes of the slice: x: 2, y: 2, z: 1, core: 2. Of those that a mesh axis runs over, the one named last changes fastest.
Arguments:
- hidden: bfloat16 [8, 1024, 1024], P('fsdp')
- positions: int32 [1024], replicated
- grad_out: bfloat16 [8, 1024, 1024], P('fsdp')
- ln_gain: bfloat16 [2, 1024], P(None, 'fsdp')
- ln_bias: bfloat16 [2, 1024], P(None, 'fsdp')
- w_query: bfloat16 [2, 1024, 16, 64], P(None, 'fsdp')
- b_query: bfloat16 [2, 1024], P(None, 'fsdp')
- w_key: bfloat16 [2, 1024, 16, 64], P(None, 'fsdp')
- b_key: bfloat16 [2, 1024], P(None, 'fsdp')
- w_value: bfloat16 [2, 1024, 16, 64], P(None, 'fsdp')
- b_value: bfloat16 [2, 1024], P(None, 'fsdp')
- w_out: bfloat16 [2, 1024, 1024], P(None, 'fsdp')
- b_out: bfloat16 [2, 1024], P(None, 'fsdp')
- w_up: bfloat16 [2, 1024, 4096], P(None, 'fsdp')
- b_up: bfloat16 [2, 4096], P(None, 'fsdp')
- w_down: bfloat16 [2, 4096, 1024], P(None, 'fsdp')
- b_down: bfloat16 [2, 1024], P(None, 'fsdp')
Outputs:
- output 1: bfloat16 [8, 1024, 1024], P('fsdp')
- output 2: bfloat16 [8, 1024, 1024], P('fsdp')
- output 3: float32 [2, 1024], P(None, 'fsdp')
- output 4: float32 [2, 1024], P(None, 'fsdp')
- output 5: float32 [2, 1024, 16, 64], P(None, 'fsdp')
- output 6: float32 [2, 1024], P(None, 'fsdp')
- output 7: float32 [2, 1024, 16, 64], P(None, 'fsdp')
- output 8: float32 [2, 1024], P(None, 'fsdp')
- output 9: float32 [2, 1024, 16, 64], P(None, 'fsdp')
- output 10: float32 [2, 1024], P(None, 'fsdp')
- output 11: float32 [2, 1024, 1024], P(None, 'fsdp')
- output 12: float32 [2, 1024], P(None, 'fsdp')
- output 13: float32 [2, 1024, 4096], P(None, 'fsdp')
- output 14: float32 [2, 4096], P(None, 'fsdp')
- output 15: float32 [2, 4096, 1024], P(None, 'fsdp')
- output 16: float32 [2, 1024], P(None, 'fsdp')
All inputs are finite; a program needn't handle non-finite values.
Results may differ from a plain program's by a relative error of at most 0.02.
Values are sent between devices in bfloat16 or wider.
A program may use at most 1 GiB of HBM per device.

v0:
```python
import functools

import jax
import jax.numpy as jnp
from jax import lax
from jax.experimental import pallas as pl
from jax.experimental.pallas import tpu as pltpu
from jax.sharding import PartitionSpec as P


ROT = 32
LN_EPS = 1e-5
THETA = 10000.0
AXIS_NAME = 'fsdp'
F32 = jnp.float32
BF16 = jnp.bfloat16
SEQ = 1024
D = 1024
FF = 4096
HEAD = 64
GROUP = 4
GW = GROUP * HEAD
STEPS = 4
QB = 256
VMEM_LIMIT = 60 * 1024 * 1024


def rope_tables(positions):
    half_rot = ROT // 2
    inv_freq = THETA ** (-2.0 * jnp.arange(half_rot, dtype=F32) / ROT)
    angles = positions.astype(F32)[:, None] * inv_freq[None, :]
    cos, sin = jnp.cos(angles), jnp.sin(angles)
    ones = jnp.ones((SEQ, HEAD - ROT), F32)
    zeros = jnp.zeros((SEQ, half_rot), F32)
    wide = jnp.zeros((SEQ, HEAD - ROT), F32)
    keep = jnp.concatenate([cos, cos, ones], axis=1)
    left = jnp.concatenate([-sin, zeros, wide], axis=1)
    right = jnp.concatenate([zeros, sin, wide], axis=1)
    return tuple(jnp.tile(t, (1, GROUP)) for t in (keep, left, right))


def head_mask(head):
    lane = lax.broadcasted_iota(jnp.int32, (1, GW), 1)
    return (lane >= head * HEAD) & (lane < (head + 1) * HEAD)


def causal_mask():
    return lax.broadcasted_iota(jnp.int32, (QB, QB), 0) <= lax.broadcasted_iota(jnp.int32, (QB, QB), 1)


def nt(a, b):
    return lax.dot_general(a, b, (((1,), (1,)), ((), ())), preferred_element_type=F32)


def nn(a, b):
    return lax.dot_general(a, b, (((1,), (0,)), ((), ())), preferred_element_type=F32)


def spin(x, keep, left, right):
    return x * keep + pltpu.roll(x, GW - ROT // 2, 1) * left + pltpu.roll(x, ROT // 2, 1) * right


def unspin(x, keep, left, right):
    return x * keep - pltpu.roll(x, GW - ROT // 2, 1) * left - pltpu.roll(x, ROT // 2, 1) * right


def attn_fwd_kernel(h_ref, wq_ref, wk_ref, wv_ref, bq_ref, bk_ref, bv_ref, keep_ref, left_ref, right_ref, qkv_ref, mixed_ref, lse_ref):
    h = h_ref[...]
    keep, left, right = keep_ref[...], left_ref[...], right_ref[...]
    q = spin(nn(h, wq_ref[...]) + bq_ref[...], keep, left, right).astype(BF16)
    qkv_ref[0] = q
    k = spin(nn(h, wk_ref[...]) + bk_ref[...], keep, left, right).astype(BF16)
    qkv_ref[1] = k
    v = nn(h, wv_ref[...]) + bv_ref[...]
    qkv_ref[2] = v.astype(BF16)
    v_t = v.T.astype(BF16)
    mask = causal_mask()
    for blk in range(SEQ // QB):
        lo, hi = blk * QB, (blk + 1) * QB
        q_blk = q[lo:hi] * jnp.asarray(HEAD ** -0.5, BF16)
        outs = []
        for head in range(GROUP):
            q_h = jnp.where(head_mask(head), q_blk, jnp.zeros_like(q_blk))
            diag = jnp.where(mask, nt(k[lo:hi], q_h), -1e30)
            top = jnp.max(diag, axis=0, keepdims=True)
            if blk:
                off = nt(k[:lo], q_h)
                top = jnp.maximum(top, jnp.max(off, axis=0, keepdims=True))
            e_diag = jnp.exp(diag - top)
            total = jnp.sum(e_diag, axis=0, keepdims=True)
            if blk:
                e_off = jnp.exp(off - top)
                total = total + jnp.sum(e_off, axis=0, keepdims=True)
            inv = 1.0 / total
            rows = slice(head * HEAD, (head + 1) * HEAD)
            out = nn(v_t[rows, lo:hi], (e_diag * inv).astype(BF16))
            if blk:
                out = out + nn(v_t[rows, :lo], (e_off * inv).astype(BF16))
            outs.append(out)
            lse_ref[0, head:head + 1, lo:hi] = top + jnp.log(total)
        mixed_ref[lo:hi, :] = jnp.concatenate(outs, axis=0).T.astype(BF16)


def attn_fwd(h, weights, biases, tables):
    full = pl.BlockSpec((SEQ, D), lambda i: (0, 0))
    table = pl.BlockSpec((SEQ, GW), lambda i: (0, 0))
    w_specs = [pl.BlockSpec((D, GW), lambda i, pos=pos: (0, pos * STEPS + i)) for pos in range(3)]
    b_spec = pl.BlockSpec((1, GW), lambda i: (0, i))
    return pl.pallas_call(
        attn_fwd_kernel,
        grid=(STEPS,),
        in_specs=[full] + w_specs + [b_spec] * 3 + [table] * 3,
        out_specs=[pl.BlockSpec((3, SEQ, GW), lambda i: (0, 0, i)), pl.BlockSpec((SEQ, GW), lambda i: (0, i)), pl.BlockSpec((1, 8, SEQ), lambda i: (i, 0, 0))],
        out_shape=[jax.ShapeDtypeStruct((3, SEQ, D), BF16), jax.ShapeDtypeStruct((SEQ, D), BF16), jax.ShapeDtypeStruct((STEPS, 8, SEQ), F32)],
        compiler_params=pltpu.CompilerParams(vmem_limit_bytes=VMEM_LIMIT),
        cost_estimate=pl.CostEstimate(flops=20_000_000_000, bytes_accessed=20_000_000, transcendentals=10_000_000),
        name='attn_fwd',
    )(h, weights, weights, weights, *biases, *tables)


def attn_bwd_kernel(qkv_ref, go_ref, lse_ref, keep_ref, left_ref, right_ref, g_ref, bias_ref, dq_acc, dk_acc, dv_acc):
    q, k, v = qkv_ref[0], qkv_ref[1], qkv_ref[2]
    k_t = k.astype(F32).T.astype(BF16)
    dk_acc[...] = jnp.zeros_like(dk_acc)
    dv_acc[...] = jnp.zeros_like(dv_acc)
    mask = causal_mask()
    scale = HEAD ** -0.5
    for blk in range(SEQ // QB):
        lo, hi = blk * QB, (blk + 1) * QB
        q_blk = q[lo:hi]
        go_blk = go_ref[lo:hi, :]
        probs, scores, q_heads, go_heads, dq_t = [], [], [], [], []
        for head in range(GROUP):
            keep_lanes = head_mask(head)
            q_h = jnp.where(keep_lanes, q_blk, jnp.zeros_like(q_blk))
            go_h = jnp.where(keep_lanes, go_blk, jnp.zeros_like(go_blk))
            lse = lse_ref[0, head:head + 1, lo:hi]
            q_s = q_h * jnp.asarray(scale, BF16)
            p = jnp.where(mask, jnp.exp(nt(k[lo:hi], q_s) - lse), 0.0)
            dp = nt(v[lo:hi], go_h)
            delta = jnp.sum(p * dp, axis=0, keepdims=True)
            if blk:
                p_off = jnp.exp(nt(k[:lo], q_s) - lse)
                dp_off = nt(v[:lo], go_h)
                delta = delta + jnp.sum(p_off * dp_off, axis=0, keepdims=True)
            ds = ((p * (dp - delta)) * scale).astype(BF16)
            p = p.astype(BF16)
            if blk:
                ds = jnp.concatenate([((p_off * (dp_off - delta)) * scale).astype(BF16), ds], axis=0)
                p = jnp.concatenate([p_off.astype(BF16), p], axis=0)
            probs.append(p)
            scores.append(ds)
            q_heads.append(q_h)
            go_heads.append(go_h)
            dq_t.append(nn(k_t[head * HEAD:(head + 1) * HEAD, :hi], ds))
        dv_acc[:hi, :] += nn(jnp.concatenate(probs, axis=1), jnp.concatenate(go_heads, axis=0))
        dk_acc[:hi, :] += nn(jnp.concatenate(scores, axis=1), jnp.concatenate(q_heads, axis=0))
        dq_acc[lo:hi, :] = jnp.concatenate(dq_t, axis=0).T
    keep, left, right = keep_ref[...], left_ref[...], right_ref[...]
    sums = []
    for pos, grad in enumerate((unspin(dq_acc[...], keep, left, right), unspin(dk_acc[...], keep, left, right), dv_acc[...])):
        g_ref[pos] = grad.astype(BF16)
        sums.append(jnp.sum(grad, axis=0, keepdims=True))
    bias_ref[...] = jnp.concatenate([jnp.concatenate(sums, axis=1), jnp.zeros((7, 3 * GW), F32)], axis=0)


def attn_bwd(qkv, grad_mixed, lse, tables):
    wide = pl.BlockSpec((3, SEQ, GW), lambda i: (0, 0, i))
    table = pl.BlockSpec((SEQ, GW), lambda i: (0, 0))
    return pl.pallas_call(
        attn_bwd_kernel,
        grid=(STEPS,),
        in_specs=[wide, pl.BlockSpec((SEQ, GW), lambda i: (0, i)), pl.BlockSpec((1, 8, SEQ), lambda i: (i, 0, 0)), table, table, table],
        out_specs=[wide, pl.BlockSpec((8, 3 * GW), lambda i: (0, i))],
        out_shape=[jax.ShapeDtypeStruct((3, SEQ, D), BF16), jax.ShapeDtypeStruct((8, 3 * D), F32)],
        scratch_shapes=[pltpu.VMEM((SEQ, GW), F32)] * 3,
        compiler_params=pltpu.CompilerParams(vmem_limit_bytes=VMEM_LIMIT),
        cost_estimate=pl.CostEstimate(flops=50_000_000_000, bytes_accessed=20_000_000, transcendentals=10_000_000),
        name='attn_bwd',
    )(qkv, grad_mixed, lse, *tables)


def wgrad_rows_kernel(core_ref, lhs_ref, lhs2_ref, rhs_ref, rhs2_ref, out_ref):
    out_ref[...] = nn(lhs_ref[...].T, rhs_ref[...]) + nn(lhs2_ref[...].T, rhs2_ref[...])


def wgrad_rows(core, lhs, lhs2, rhs, rhs2):
    tile = 256
    lhs_spec = pl.BlockSpec((SEQ, tile), lambda i, c: (0, (i // 2) * 4 + c[0] * 2 + i % 2))
    rhs_spec = pl.BlockSpec((SEQ, D), lambda i, c: (0, 0))
    return pl.pallas_call(
        wgrad_rows_kernel,
        grid_spec=pltpu.PrefetchScalarGridSpec(
            num_scalar_prefetch=1,
            grid=(FF // 2 // tile,),
            in_specs=[lhs_spec, lhs_spec, rhs_spec, rhs_spec],
            out_specs=pl.BlockSpec((tile, D), lambda i, c: (i, 0)),
        ),
        out_shape=jax.ShapeDtypeStruct((FF // 2, D), F32),
        compiler_params=pltpu.CompilerParams(vmem_limit_bytes=VMEM_LIMIT),
        cost_estimate=pl.CostEstimate(flops=2 * FF * D * SEQ, bytes_accessed=20_000_000, transcendentals=0),
        name='wgrad_rows',
    )(core, lhs, lhs2, rhs, rhs2)


TILE = 512


def segment_tiles(rhs):
    return rhs.size // (SEQ * TILE)


def wgrad_cols_kernel(plan, *refs):
    lefts = sorted({p[0] for p in plan}, reverse=False)
    n_left = 8 * len(lefts)
    rhs_refs = refs[1 + n_left:1 + n_left + 2 * len(plan)]
    out_ref, left = refs[-2], refs[-1]
    step = pl.program_id(0)
    loaded = None
    for seg, (which, first, last) in enumerate(plan):
        if which != loaded:
            blocks = refs[1 + 8 * lefts.index(which):1 + 8 * lefts.index(which) + 8]
            loaded = which

            @pl.when(step == first)
            def _(blocks=blocks):
                for j in range(4):
                    left[128 * j:128 * (j + 1), :SEQ] = blocks[j][...].T
                    left[128 * j:128 * (j + 1), SEQ:] = blocks[4 + j][...].T

        here, there = rhs_refs[2 * seg], rhs_refs[2 * seg + 1]

        @pl.when((step >= first) & (step < last))
        def _(here=here, there=there):
            a, b = (here[0], there[0]) if len(here.shape) == 3 else (here[...], there[...])
            out_ref[...] = nn(left[:, :SEQ], a) + nn(left[:, SEQ:], b)


def wgrad_cols(core, lefts, segments):
    plan, specs, args, first = [], [], [], 0
    for mine, partner in lefts:
        for values in (mine, partner):
            for j in range(4):
                specs.append(pl.BlockSpec((SEQ, 128), lambda i, c, j=j: (0, 2 * j + c[0])))
                args.append(values)
    for which, mine, partner in segments:
        tiles = segment_tiles(mine)

        def place(i, c, first=first, tiles=tiles, deep=mine.ndim == 3):
            pos = jnp.clip(i - first, 0, tiles - 1)
            return (pos // 2, 0, pos % 2) if deep else (0, pos)

        shape = (1, SEQ, TILE) if mine.ndim == 3 else (SEQ, TILE)
        specs += [pl.BlockSpec(shape, place)] * 2
        args += [mine, partner]
        plan.append((which, first, first + tiles))
        first += tiles
    return pl.pallas_call(
        functools.partial(wgrad_cols_kernel, tuple(plan)),
        grid_spec=pltpu.PrefetchScalarGridSpec(
            num_scalar_prefetch=1,
            grid=(first,),
            in_specs=specs,
            out_specs=pl.BlockSpec((D // 2, TILE), lambda i, c: (0, i)),
            scratch_shapes=[pltpu.VMEM((D // 2, 2 * SEQ), BF16)],
        ),
        out_shape=jax.ShapeDtypeStruct((D // 2, first * TILE), F32),
        compiler_params=pltpu.CompilerParams(vmem_limit_bytes=VMEM_LIMIT),
        cost_estimate=pl.CostEstimate(flops=2 * SEQ * D * first * TILE, bytes_accessed=3_200_000 * first, transcendentals=0),
        name='wgrad_cols',
    )(core, *args)


def unpack_kernel(scale, *refs):
    srcs, outs = refs[:5], refs[-5:]
    step = pl.program_id(0)
    for slot in range(3):
        @pl.when(step == slot)
        def _(slot=slot):
            outs[slot][0] = (srcs[slot][...] * scale).T

    @pl.when((step >= 3) & (step < 7))
    def _():
        outs[3][0] = srcs[3][...] * scale

    @pl.when(step == 7)
    def _():
        outs[4][0] = srcs[4][...] * scale


def unpack(sources, layer, scale, previous=None):
    def col(i):
        return jnp.clip(i - 3, 0, 3)

    in_specs = []
    for slot, (_, base) in enumerate(sources):
        if slot == 3:
            in_specs.append(pl.BlockSpec((128, D), lambda i, base=base: (0, base + col(i))))
        else:
            in_specs.append(pl.BlockSpec((128, D), lambda i, base=base: (0, base)))
    args = [src for src, _ in sources]
    aliases = {}
    if previous is not None:
        in_specs += [pl.BlockSpec(memory_space=pl.ANY)] * 5
        args += list(previous)
        aliases = {5 + i: i for i in range(5)}
    turned = pl.BlockSpec((1, D, 128), lambda i: (layer, 0, 0))
    return pl.pallas_call(
        functools.partial(unpack_kernel, scale),
        grid=(8,),
        in_specs=in_specs,
        out_specs=[turned] * 3 + [pl.BlockSpec((1, 128, D), lambda i: (layer, 0, col(i))), pl.BlockSpec((1, 128, D), lambda i: (layer, 0, 0))],
        out_shape=[jax.ShapeDtypeStruct((2, D, 128), F32)] * 3 + [jax.ShapeDtypeStruct((2, 128, FF), F32), jax.ShapeDtypeStruct((2, 128, D), F32)],
        input_output_aliases=aliases,
        compiler_params=pltpu.CompilerParams(vmem_limit_bytes=VMEM_LIMIT),
        cost_estimate=pl.CostEstimate(flops=2_000_000, bytes_accessed=8_400_000, transcendentals=0),
        name='unpack',
    )(*args)


def stack_blocks(ref):
    return jnp.concatenate([ref[:, b * D:(b + 1) * D] for b in range(4)], axis=0)


def finish_kernel(base_ref, act_ref, wdown_ref, bd_ref, out_ref, acc):
    step = pl.program_id(0)

    @pl.when(step == 0)
    def _():
        acc[...] = base_ref[...]

    acc[...] += nn(act_ref[...], stack_blocks(wdown_ref))

    @pl.when(step == FF // TILE - 1)
    def _():
        out_ref[...] = (acc[...] + bd_ref[...]).astype(BF16)


def finish(base, act, down_from, bd):
    full = pl.BlockSpec((SEQ, D), lambda i: (0, 0))
    return pl.pallas_call(
        finish_kernel,
        grid=(FF // TILE,),
        in_specs=[full, pl.BlockSpec((SEQ, TILE), lambda i: (0, i)), pl.BlockSpec((128, 4 * D), lambda i: (i, down_from[1])), pl.BlockSpec((1, D), lambda i: (0, 0))],
        out_specs=full,
        out_shape=jax.ShapeDtypeStruct((SEQ, D), BF16),
        scratch_shapes=[pltpu.VMEM((SEQ, D), F32)],
        compiler_params=pltpu.CompilerParams(vmem_limit_bytes=VMEM_LIMIT),
        cost_estimate=pl.CostEstimate(flops=2 * SEQ * D * FF, bytes_accessed=26_000_000, transcendentals=0),
        name='finish',
    )(base, act, down_from[0], bd)


def mlp_pull_kernel(grad_ref, wdown_ref, pre_ref, out_ref, bias_ref):
    root = 0.7978845608028654
    weight = stack_blocks(wdown_ref)
    total = jnp.zeros((8, TILE), F32)
    for base in range(0, SEQ, 256):
        upstream = nt(grad_ref[base:base + 256, :], weight).astype(BF16)
        for low in range(0, 256, 32):
            x = pre_ref[base + low:base + low + 32, :]
            square = x * x
            t = jnp.tanh(x * (root + (root * 0.044715) * square))
            slope = 0.5 * (1.0 + t) + (0.5 * x) * ((1.0 - t * t) * (root + (root * 3 * 0.044715) * square))
            grad = upstream[low:low + 32].astype(F32) * slope
            out_ref[base + low:base + low + 32, :] = grad.astype(BF16)
            total += jnp.sum(grad.reshape(4, 8, TILE), axis=0)
    bias_ref[...] = total


def mlp_pull(grad, down_from, up_pre):
    full = pl.BlockSpec((SEQ, D), lambda i: (0, 0))
    tile = pl.BlockSpec((SEQ, TILE), lambda i: (0, i))
    pre, bias = pl.pallas_call(
        mlp_pull_kernel,
        grid=(FF // TILE,),
        in_specs=[full, pl.BlockSpec((128, 4 * D), lambda i: (i, down_from[1])), tile],
        out_specs=[tile, pl.BlockSpec((8, TILE), lambda i: (0, i))],
        out_shape=[jax.ShapeDtypeStruct((SEQ, FF), BF16), jax.ShapeDtypeStruct((8, FF), F32)],
        compiler_params=pltpu.CompilerParams(vmem_limit_bytes=VMEM_LIMIT),
        cost_estimate=pl.CostEstimate(flops=2 * SEQ * D * FF, bytes_accessed=36_000_000, transcendentals=SEQ * FF),
        name='mlp_pull',
    )(grad, down_from[0], up_pre)
    return pre, jnp.sum(bias, axis=0)


def join_kernel(q_ref, k_ref, v_ref, up_ref, out_w_ref, joined_ref):
    step = pl.program_id(0)
    for slot, ref in enumerate((q_ref, k_ref, v_ref)):
        @pl.when(step == slot)
        def _(ref=ref):
            joined_ref[...] = ref[0].T

    @pl.when((step >= 3) & (step < 7))
    def _():
        joined_ref[...] = up_ref[0]

    @pl.when(step == 7)
    def _():
        joined_ref[...] = out_w_ref[0]


def join(w_query, w_key, w_value, w_up, w_out, layer):
    turned = [w.transpose(0, 2, 3, 1).reshape(2, D, 128) for w in (w_query, w_key, w_value)]
    turned_spec = pl.BlockSpec((1, D, 128), lambda i: (layer, 0, 0))
    return pl.pallas_call(
        join_kernel,
        grid=(8,),
        in_specs=[turned_spec] * 3 + [pl.BlockSpec((1, 128, D), lambda i: (layer, 0, jnp.clip(i - 3, 0, 3))), pl.BlockSpec((1, 128, D), lambda i: (layer, 0, 0))],
        out_specs=pl.BlockSpec((128, D), lambda i: (0, i)),
        out_shape=jax.ShapeDtypeStruct((128, 8 * D), BF16),
        cost_estimate=pl.CostEstimate(flops=1_000_000, bytes_accessed=4_200_000, transcendentals=0),
        name='join',
    )(*turned, w_up, w_out)


def gelu_tanh(values):
    return jax.nn.gelu(values, approximate=True)


def layer_norm(hidden, gain, bias):
    tok = hidden.astype(F32)
    centred = tok - jnp.mean(tok, axis=-1, keepdims=True)
    inv_std = lax.rsqrt(jnp.mean(centred * centred, axis=-1, keepdims=True) + LN_EPS)
    normed = centred * inv_std
    return normed, inv_std, (normed * gain + bias).astype(BF16)


def bar(*values):
    return lax.optimization_barrier(values)


def solution(mesh):
    group_size = mesh.shape[AXIS_NAME]
    batch_spec = P(AXIS_NAME)
    param_specs = (P(None, AXIS_NAME),) * 14
    swap = [(i, i ^ 1) for i in range(group_size)]
    chips = [[i for i in range(group_size) if i % 2 == c] for c in range(2)]

    def exchange(values):
        return lax.ppermute(values, AXIS_NAME, swap)

    def hop(values, offset):
        return lax.ppermute(values, AXIS_NAME, [(i, i ^ offset) for i in range(group_size)])

    def gather(values):
        return lax.all_gather(values, AXIS_NAME, axis=0, tiled=True)

    def scatter(values):
        return lax.psum_scatter(values, AXIS_NAME, scatter_dimension=0, axis_index_groups=chips, tiled=True)

    def step(hidden, positions, grad_out, *shards):
        (ln_gain, ln_bias, w_query, b_query, w_key, b_key, w_value, b_value, w_out, b_out, w_up, b_up, w_down, b_down) = shards
        layers = ln_gain.shape[0]
        token_total = hidden.shape[0] * hidden.shape[1] * group_size
        rank = lax.axis_index(AXIS_NAME)
        core = lax.rem(rank, 2)
        core_arr = core.reshape(1).astype(jnp.int32)
        tables = rope_tables(positions)

        def rows(w, layer):
            return w[layer].reshape(w.shape[1], -1)

        def blocks(layer):
            return [w_down[layer, b * 128:(b + 1) * 128] for b in range(4)]

        wide0 = gather(join(w_query, w_key, w_value, w_up, w_out, 0))
        second = gather(jnp.concatenate([rows(w_up, 1)] + blocks(0), axis=1))
        third = gather(jnp.concatenate([rows(w, 1) for w in (w_query, w_key, w_value, w_out)] + blocks(1), axis=1))

        small = jnp.concatenate([b.reshape(layers, -1) for b in (ln_gain, ln_bias, b_query, b_key, b_value, b_out, b_down, b_up)], axis=1)
        small = gather(small[None])

        def split(layer):
            mine = small[:, layer]
            vecs = [mine[:, i * 128:(i + 1) * 128].reshape(1, D).astype(F32) for i in range(7)]
            return vecs + [mine[:, 7 * 128:].reshape(1, FF).astype(F32)]

        def mlp_up(h, wup, bu):
            up_pre = nn(h, wup) + bu
            return up_pre, gelu_tanh(up_pre).astype(BF16)

        def norm_pull(grad, grad_normed, normed, inv_std, gain):
            grad_hat = grad_normed * gain
            grad_in = inv_std * (grad_hat - jnp.mean(grad_hat, axis=-1, keepdims=True) - normed * jnp.mean(grad_hat * normed, axis=-1, keepdims=True))
            return (grad.astype(F32) + grad_in).astype(BF16), jnp.sum(grad_normed * normed, axis=0), jnp.sum(grad_normed, axis=0)

        def back_qkv(g, weights, slots=(0, 1, 2)):
            return sum(nt(g[pos], weights[:, pos * D:(pos + 1) * D]) for pos in slots)

        along_x, along_y = lax.rem(rank // 2, 2), rank // 4

        def pick(values, index, axis):
            return lax.dynamic_index_in_dim(values, index, axis, keepdims=False)

        def ring_send(dw):
            parts = dw.reshape(2, 2, 2, dw.shape[0] // 8, dw.shape[1])
            first, second = parts[:, :, 0], parts[:, :, 1]
            send_first, send_second = pick(first, 1 - along_x, 1), pick(second, 1 - along_y, 0)
            got_first = hop(send_first, 2)
            got_second = hop(send_second, 4)
            return first, second, got_first, got_second

        def ring_turn(first, second, got_first, got_second):
            sum_first = pick(first, along_x, 1) + got_first
            sum_second = pick(second, along_y, 0) + got_second
            kept = pick(sum_first, along_y, 0), pick(sum_second, along_x, 0)
            return kept + (hop(pick(sum_first, 1 - along_y, 0), 4), hop(pick(sum_second, 1 - along_x, 0), 2))

        def ring_end(kept_first, kept_second, got_first, got_second):
            return jnp.concatenate([kept_first + got_first, kept_second + got_second], axis=0)

        def pack(g_gain, g_lbias, g_bias, grad, g_b_up):
            g_bias = g_bias[0].reshape(STEPS, 3, GW)
            pieces = [g_gain, g_lbias] + [g_bias[:, i].reshape(D) for i in range(3)] + [jnp.sum(grad.astype(F32), axis=0)]
            return jnp.concatenate([p.reshape(8, 128) for p in pieces] + [g_b_up.reshape(8, 512)], axis=1)

        up_cols = slice(3 * D, 3 * D + FF)
        out_cols = slice(3 * D + FF, 4 * D + FF)

        def base_sum(x, mixed, wout, bo):
            return x.astype(F32) + nn(mixed, wout) + bo

        x0 = hidden.reshape(SEQ, D)
        gain0, lbias0, bq, bk, bv, bo, bd, bu = split(0)
        normed0, inv0, h0 = layer_norm(x0, gain0, lbias0)
        qkv0, mixed0, lse0 = attn_fwd(h0, wide0, (bq, bk, bv), tables)
        mixed0, h0_a = bar(mixed0, h0)
        up_pre0, act0 = mlp_up(h0_a, wide0[:, up_cols], bu)
        base0, act0 = bar(base_sum(x0, mixed0, wide0[:, out_cols], bo), act0)
        x1 = finish(base0, act0, (second, 1), bd)
        h0x, act0x, mixed0x = exchange(h0), exchange(act0), exchange(mixed0)

        top = grad_out.reshape(SEQ, D)
        topx = exchange(top)
        gain1, lbias1, bq, bk, bv, bo1, bd1, bu = split(1)
        normed1, inv1, h1 = layer_norm(x1, gain1, lbias1)
        up_pre1, act1 = mlp_up(h1, second[:, :FF], bu)
        h1x, act1x = exchange(h1), exchange(act1)
        dw, top_a = bar(wgrad_rows(core_arr, act1, act1x, top, topx), top)
        rs_down1 = scatter(dw)
        pre1, g_bup1 = mlp_pull(top_a, (third, 1), up_pre1)
        pre1x = exchange(pre1)
        pre1_a, h1_a = bar(pre1, h1)
        qkv1, mixed1, lse1 = attn_fwd(h1_a, third, (bq, bk, bv), tables)
        mixed1, pre1_b = bar(mixed1, pre1_a)
        mixed1x = exchange(mixed1)
        dw, top_b = bar(wgrad_cols(core_arr, [(h1, h1x)], [(0, pre1_b, pre1x)]), top_a)
        rs_up1 = scatter(dw)
        g1, g_bias1 = attn_bwd(qkv1, nt(top_b, third[:, 3 * D:4 * D]).astype(BF16), lse1, tables)
        g1x = exchange(g1)
        g1_b, back1 = bar(g1, back_qkv(g1, third, (0, 1)))
        dw, g1_c, back1, pre1_c = bar(wgrad_cols(core_arr, [(h1, h1x), (mixed1, mixed1x)], [(0, g1_b, g1x), (1, top, topx)]), g1_b, back1, pre1_b)
        rs_qkvo1 = scatter(dw)
        mid, g_gain, g_lbias = norm_pull(top, back1 + back_qkv(g1_c, third, (2,)) + nt(pre1_c, second[:, :FF]), normed1, inv1, gain1)
        little1 = pack(g_gain, g_lbias, g_bias1, top, g_bup1)

        midx = exchange(mid)
        pre0, g_bup0 = mlp_pull(mid, (second, 1), up_pre0)
        pre0x = exchange(pre0)
        pre0_a, mid_a = bar(pre0, mid)
        sent = ring_send(wgrad_rows(core_arr, act0, act0x, mid_a, midx))
        first, second_half, got_first, got_second = sent
        first, second_half, mid_b, pre0_b = bar(first, second_half, mid_a, pre0_a)
        sent = (first, second_half, got_first, got_second)
        go0 = nt(mid_b, wide0[:, out_cols]).astype(BF16)
        dw = wgrad_cols(core_arr, [(h0, h0x)], [(0, pre0_b, pre0x)])
        dw, go0 = bar(dw, go0)
        rs_up0 = scatter(dw)
        g0, g_bias0 = attn_bwd(qkv0, go0, lse0, tables)
        g0x = exchange(g0)
        *sent, g0_a, pre0_c = bar(*sent, g0, pre0_b)
        turned = ring_turn(*sent)
        g0_b, back0 = bar(g0_a, nt(pre0_c, wide0[:, up_cols]))
        dw = wgrad_cols(core_arr, [(h0, h0x), (mixed0, mixed0x)], [(0, g0_b, g0x), (1, mid_b, midx)])
        dw, g0_c, back0, mixed1_b, act1_b = bar(dw, g0_b, back0, mixed1, act1)
        rs_qkvo0 = scatter(dw)
        grad, g_gain, g_lbias = norm_pull(mid, back0 + back_qkv(g0_c, wide0), normed0, inv0, gain0)
        *turned, grad = bar(*turned, grad)
        rs_down0 = ring_end(*turned)
        little0 = pack(g_gain, g_lbias, g_bias0, mid, g_bup0)
        current = finish(base_sum(x1, mixed1_b, third[:, 3 * D:4 * D], bo1), act1_b, (third, 1), bd1)
        little = [little0, little1]

        scale = 1.0 / token_total
        everyone = gather(jnp.stack(little, axis=1)[None])
        own = jnp.sum(lax.dynamic_index_in_dim(everyone, rank, 1, keepdims=False), axis=0) * scale
        vec = [own[:, i * 128:(i + 1) * 128] for i in range(6)]

        done = unpack([(rs_qkvo1, 0), (rs_qkvo1, 1), (rs_qkvo1, 2), (rs_up1, 0), (rs_qkvo1, 3)], 1, scale)
        done = unpack([(rs_qkvo0, 0), (rs_qkvo0, 1), (rs_qkvo0, 2), (rs_up0, 0), (rs_qkvo0, 3)], 0, scale, done)
        g_query, g_key, g_value = [g.reshape(layers, 16, HEAD, 128).transpose(0, 3, 1, 2) for g in done[:3]]

        return (current.reshape(hidden.shape), grad.reshape(hidden.shape), vec[0], vec[1],
                g_query, vec[2], g_key, vec[3], g_value, vec[4],
                done[4], vec[5],
                done[3], own[:, 6 * 128:], jnp.stack([rs_down0 * scale, rs_down1 * scale]), vec[5])

    return jax.shard_map(step, mesh=mesh, in_specs=(batch_spec, P(), batch_spec) + param_specs, out_specs=(batch_spec, batch_spec) + param_specs, check_vma=False)
```

profile of v0, /device:TPU:0, one launch (start us, length us, event | category | flops | bytes accessed | tf_op | source)
XLA Modules:
  0.0 845.8 jit_solution(17554583268565534269)
XLA Ops:
  51.8 48.2 %all-gather.7.cloned.1.call-done.wq_ref.wk_ref.wv_ref = bf16[1024,8192]{1,0:T(8,128)(2,1)} async-done(((bf16[128,8192]{1,0:T(8,128)(2,1)}), bf16[1024,8192]{1,0:T(8,128)(2,1)}) %all-gather.7.cloned.1.call-update) | async-done | bytes 16777232 | tf_op jit(solution)/shard_map/all_gather | solution.py:447
  100.1 46.6 %attn_fwd.2 = (bf16[3,1024,1024]{2,1,0:T(8,128)(2,1)}, bf16[1024,1024]{1,0:T(8,128)(2,1)}, f32[4,8,1024]{2,1,0:T(8,128)}) custom-call(bf16[1024,1024]{1,0:T(8,128)(2,1)} %fusion.44.h_ref.refs_1_.refs_2_.refs_3_.refs_4_, bf16[1024,8192]{1,0:T(8,128)(2,1)} %all-gather.7.cloned.1.call-done.wq_ref.wk_ref.wv_ref, ...), custom_call_target="tpu_custom_call" | custom-call | flops 20000000000 | bytes 20000000 | tf_op jit(solution)/shard_map/attn_fwd/pallas_call | solution.py:109
  153.5 19.1 %fusion.7 = (bf16[1024,4096]{1,0:T(8,128)(2,1)}, f32[1024,4096]{1,0:T(8,128)}) fusion(f32[4096]{0:T(1024)S(1)} %bitcast.236, bf16[1024,1024]{1,0:T(8,128)(2,1)S(1)} %copy-done, bf16[1024,8192]{1,0:T(8,128)(2,1)} %all-gather.7.cloned.1.call-done.wq_ref.wk_ref.wv_ref), kind=kOutput, calls=%fused_computation.9 | convolution fusion | flops 8631877632 | bytes 35667968 | tf_op jit(solution)/shard_map/dot_general | solution.py:56
  186.1 16.4 %finish.2 = bf16[1024,1024]{1,0:T(8,128)(2,1)} custom-call(f32[1024,1024]{1,0:T(8,128)} %fusion.50.base_ref, bf16[1024,4096]{1,0:T(8,128)(2,1)} %get-tuple-element.88.act_ref.lhs_ref, bf16[1024,8192]{1,0:T(8,128)(2,1)} %all-gather.9.cloned.1.call-done.wdown_ref, f32[1,1024]{1,0:T(1,128)} %bitcast.248), custom_call_target="tpu_custom_call" | custom-call | flops 8589934592 | bytes 26000000 | tf_op jit(solution)/shard_map/finish/pallas_call | solution.py:341
  207.8 21.3 %fusion.15 = (bf16[1024,4096]{1,0:T(8,128)(2,1)}, f32[1024,4096]{1,0:T(8,128)}) fusion(f32[4096]{0:T(1024)S(1)} %bitcast.235, bf16[1024,1024]{1,0:T(8,128)(2,1)S(1)} %fusion.37.h_ref.refs_1_.refs_2_.refs_3_.refs_4_, bf16[1024,8192]{1,0:T(8,128)(2,1)} %all-gather.9.cloned.1.call-done.wdown_ref), kind=kOutput, calls=%fused_computation.17 | convolution fusion | flops 8631877632 | bytes 35667968 | tf_op jit(solution)/shard_map/dot_general | solution.py:56
  229.6 17.9 %collective-permute-done.5.rhs2_ref.refs_20_ = bf16[1024,1024]{1,0:T(8,128)(2,1)} collective-permute-done((bf16[1024,1024]{1,0:T(8,128)(2,1)}, bf16[1024,1024]{1,0:T(8,128)(2,1)}, u32[]{:S(2)}, u32[]{:S(2)}) %collective-permute-start.5) | collective-permute-done | bytes 2097184 | tf_op jit(solution)/shard_map/ppermute | solution.py:441
  247.5 15.2 %wgrad_rows.2 = f32[2048,1024]{1,0:T(8,128)} custom-call(s32[1]{0:T(128)} %bitcast.24.core_ref.refs_0_, bf16[1024,4096]{1,0:T(8,128)(2,1)} %get-tuple-element.121.lhs_ref.act_ref, bf16[1024,4096]{1,0:T(8,128)(2,1)} %collective-permute-done.4.lhs2_ref, bf16[1024,1024]{1,0:T(8,128)(2,1)} %bitcast.25.rhs_ref.grad_ref.refs_19_, ...), custom_call_target="tpu_custom_call" | custom-call | flops 8589934592 | bytes 20000000 | tf_op jit(solution)/shard_map/wgrad_rows/pallas_call | solution.py:191
  272.7 22.5 %mlp_pull.2 = (bf16[1024,4096]{1,0:T(8,128)(2,1)}, f32[8,4096]{1,0:T(8,128)}) custom-call(bf16[1024,1024]{1,0:T(8,128)(2,1)} %bitcast.25.rhs_ref.grad_ref.refs_19_, bf16[1024,8192]{1,0:T(8,128)(2,1)} %all-gather.11.cloned.1.call-done.wdown_ref.wq_ref.wk_ref.wv_ref, f32[1024,4096]{1,0:T(8,128)} %get-tuple-element.217.pre_ref), custom_call_target="tpu_custom_call" | custom-call | flops 8589934592 | bytes 36000000 | tf_op jit(solution)/shard_map/mlp_pull/pallas_call | solution.py:374
  295.7 46.5 %attn_fwd.3 = (bf16[3,1024,1024]{2,1,0:T(8,128)(2,1)}, bf16[1024,1024]{1,0:T(8,128)(2,1)}, f32[4,8,1024]{2,1,0:T(8,128)}) custom-call(bf16[1024,1024]{1,0:T(8,128)(2,1)} %copy-done.2, bf16[1024,8192]{1,0:T(8,128)(2,1)} %all-gather.11.cloned.1.call-done.wdown_ref.wq_ref.wk_ref.wv_ref, ...), custom_call_target="tpu_custom_call" | custom-call | flops 20000000000 | bytes 20000000 | tf_op jit(solution)/shard_map/attn_fwd/pallas_call | solution.py:109
  342.1 16.6 %wgrad_cols.4 = f32[512,4096]{1,0:T(8,128)} custom-call(s32[1]{0:T(128)} %bitcast.24.core_ref.refs_0_, bf16[1024,1024]{1,0:T(8,128)(2,1)} %copy-done.2, bf16[1024,1024]{1,0:T(8,128)(2,1)} %copy-done.2, bf16[1024,1024]{1,0:T(8,128)(2,1)} %copy-done.2, bf16[1024,1024]{1,0:T(8,128)(2,1)} %copy-done.2, ...), custom_call_target="tpu_custom_call" | custom-call | flops 8589934592 | bytes 25600000 | tf_op jit(solution)/shard_map/wgrad_cols/pallas_call | solution.py:258
  364.9 48.2 %attn_bwd.2 = (bf16[3,1024,1024]{2,1,0:T(8,128)(2,1)}, f32[8,3072]{1,0:T(8,128)}) custom-call(bf16[3,1024,1024]{2,1,0:T(8,128)(2,1)} %get-tuple-element.95.qkv_ref, bf16[1024,1024]{1,0:T(8,128)(2,1)} %convolution_convert_fusion.1.go_ref, f32[4,8,1024]{2,1,0:T(8,128)} %get-tuple-element.98.lse_ref, f32[1024,256]{1,0:T(8,128)} %copy.106.keep_ref, ...), custom_call_target="tpu_custom_call" | custom-call | flops 49999998976 | bytes 20000000 | tf_op jit(solution)/shard_map/attn_bwd/pallas_call | solution.py:170
  427.8 18.7 %wgrad_cols.5 = f32[512,4096]{1,0:T(8,128)} custom-call(s32[1]{0:T(128)} %bitcast.24.core_ref.refs_0_, bf16[1024,1024]{1,0:T(8,128)(2,1)} %copy-done.2, bf16[1024,1024]{1,0:T(8,128)(2,1)} %copy-done.2, bf16[1024,1024]{1,0:T(8,128)(2,1)} %copy-done.2, bf16[1024,1024]{1,0:T(8,128)(2,1)} %copy-done.2, ...), custom_call_target="tpu_custom_call" | custom-call | flops 8589934592 | bytes 25600000 | tf_op jit(solution)/shard_map/wgrad_cols/pallas_call | solution.py:258
  453.4 16.5 %fusion.41 = (f32[1024]{0:T(1024)S(1)}, f32[1024]{0:T(1024)S(1)}, f32[1024]{0:T(1024)S(1)}, f32[1024]{0:T(1024)S(1)}, f32[1024,1024]{1,0:T(8,128)S(1)}) fusion(bf16[1024,1024]{1,0:T(8,128)(2,1)S(1)} %copy-done.13, f32[1024]{0:T(1024)S(1)} %copy-done.35, f32[1024]{0:T(1024)S(1)} %copy-done.31, f32[1024]{0:T(1024)S(1)} %copy-done.37, ...), kind=kOutput, calls=%fused_computation.54 | convolution fusion | flops 8602513408 | bytes 31485952 | tf_op jit(solution)/shard_map/dot_general | solution.py:52
  475.0 21.9 %mlp_pull.3 = (bf16[1024,4096]{1,0:T(8,128)(2,1)}, f32[8,4096]{1,0:T(8,128)}) custom-call(bf16[1024,1024]{1,0:T(8,128)(2,1)} %get-tuple-element.112.grad_ref.rhs_ref.refs_19_, bf16[1024,8192]{1,0:T(8,128)(2,1)} %all-gather.9.cloned.1.call-done.wdown_ref, f32[1024,4096]{1,0:T(8,128)} %get-tuple-element.215.pre_ref), custom_call_target="tpu_custom_call" | custom-call | flops 8589934592 | bytes 36000000 | tf_op jit(solution)/shard_map/mlp_pull/pallas_call | solution.py:374
  497.9 15.6 %collective-permute-done.9.rhs2_ref.refs_20_ = bf16[1024,1024]{1,0:T(8,128)(2,1)} collective-permute-done((bf16[1024,1024]{1,0:T(8,128)(2,1)}, bf16[1024,1024]{1,0:T(8,128)(2,1)}, u32[]{:S(2)}, u32[]{:S(2)}) %collective-permute-start.9) | collective-permute-done | bytes 2097184 | tf_op jit(solution)/shard_map/ppermute | solution.py:441
  513.5 15.0 %wgrad_rows.3 = f32[2048,1024]{1,0:T(8,128)} custom-call(s32[1]{0:T(128)} %bitcast.24.core_ref.refs_0_, bf16[1024,4096]{1,0:T(8,128)(2,1)} %get-tuple-element.88.act_ref.lhs_ref, bf16[1024,4096]{1,0:T(8,128)(2,1)} %collective-permute-done.2.lhs2_ref, bf16[1024,1024]{1,0:T(8,128)(2,1)} %get-tuple-element.112.grad_ref.rhs_ref.refs_19_, ...), custom_call_target="tpu_custom_call" | custom-call | flops 8589934592 | bytes 20000000 | tf_op jit(solution)/shard_map/wgrad_rows/pallas_call | solution.py:191
  544.7 16.6 %wgrad_cols.6 = f32[512,4096]{1,0:T(8,128)} custom-call(s32[1]{0:T(128)} %bitcast.24.core_ref.refs_0_, bf16[1024,1024]{1,0:T(8,128)(2,1)} %fusion.44.h_ref.refs_1_.refs_2_.refs_3_.refs_4_, bf16[1024,1024]{1,0:T(8,128)(2,1)} %fusion.44.h_ref.refs_1_.refs_2_.refs_3_.refs_4_, bf16[1024,1024]{1,0:T(8,128)(2,1)} %fusion.44.h_ref.refs_1_.refs_2_.refs_3_.refs_4_, ...), custom_call_target="tpu_custom_call" | custom-call | flops 8589934592 | bytes 25600000 | tf_op jit(solution)/shard_map/wgrad_cols/pallas_call | solution.py:258
  561.4 47.9 %attn_bwd.3 = (bf16[3,1024,1024]{2,1,0:T(8,128)(2,1)}, f32[8,3072]{1,0:T(8,128)}) custom-call(bf16[3,1024,1024]{2,1,0:T(8,128)(2,1)} %get-tuple-element.110.qkv_ref, bf16[1024,1024]{1,0:T(8,128)(2,1)} %convolution_convert_fusion.go_ref, f32[4,8,1024]{2,1,0:T(8,128)} %get-tuple-element.114.lse_ref, f32[1024,256]{1,0:T(8,128)} %copy.106.keep_ref, ...), custom_call_target="tpu_custom_call" | custom-call | flops 49999998976 | bytes 20000000 | tf_op jit(solution)/shard_map/attn_bwd/pallas_call | solution.py:170
  613.6 68.4 %collective-permute-done.10 = f32[2,256,1024]{2,1,0:T(8,128)} collective-permute-done((f32[2,256,1024]{2,1,0:T(8,128)S(1)}, f32[2,256,1024]{2,1,0:T(8,128)}, u32[]{:S(2)}, u32[]{:S(2)}) %collective-permute-start.10) | collective-permute-done | bytes 2097184 | tf_op jit(solution)/shard_map/ppermute | solution.py:444
  683.1 15.2 %fusion.19 = f32[1024,1024]{1,0:T(8,128)} fusion(bf16[1024,4096]{1,0:T(8,128)(2,1)} %get-tuple-element.117.refs_9_, bf16[1024,8192]{1,0:T(8,128)(2,1)} %all-gather.7.cloned.1.call-done.wq_ref.wk_ref.wv_ref), kind=kOutput, calls=%fused_computation.23 | convolution fusion | flops 8589934592 | bytes 20971520 | tf_op jit(solution)/shard_map/dot_general | solution.py:52
  699.7 18.5 %wgrad_cols.7 = f32[512,4096]{1,0:T(8,128)} custom-call(s32[1]{0:T(128)} %bitcast.24.core_ref.refs_0_, bf16[1024,1024]{1,0:T(8,128)(2,1)} %fusion.44.h_ref.refs_1_.refs_2_.refs_3_.refs_4_, bf16[1024,1024]{1,0:T(8,128)(2,1)} %fusion.44.h_ref.refs_1_.refs_2_.refs_3_.refs_4_, bf16[1024,1024]{1,0:T(8,128)(2,1)} %fusion.44.h_ref.refs_1_.refs_2_.refs_3_.refs_4_, ...), custom_call_target="tpu_custom_call" | custom-call | flops 8589934592 | bytes 25600000 | tf_op jit(solution)/shard_map/wgrad_cols/pallas_call | solution.py:258
  751.4 23.7 %collective-permute-done.14 = f32[256,1024]{1,0:T(8,128)S(1)} collective-permute-done((f32[256,1024]{1,0:T(8,128)}, f32[256,1024]{1,0:T(8,128)S(1)}, u32[]{:S(2)}, u32[]{:S(2)}) %collective-permute-start.14) | collective-permute-done | bytes 1048608 | tf_op jit(solution)/shard_map/ppermute | solution.py:444
  779.6 15.7 %all-gather.1 = f32[64,2,1280]{2,0,1:T(8,128)S(1)} all-gather(f32[8,2,1280]{2,0,1:T(8,128)S(1)} %pad_maximum_fusion.1), channel_id=3, replica_groups=mesh['fsdp'=8] {'fsdp'}, dimensions={0}, use_global_device_ids=true | all-gather | bytes 737280 | tf_op jit(solution)/shard_map/all_gather | solution.py:447
  808.1 16.1 %finish.3 = bf16[1024,1024]{1,0:T(8,128)(2,1)} custom-call(f32[1024,1024]{1,0:T(8,128)} %fusion.53.base_ref, bf16[1024,4096]{1,0:T(8,128)(2,1)} %get-tuple-element.121.lhs_ref.act_ref, bf16[1024,8192]{1,0:T(8,128)(2,1)} %all-gather.11.cloned.1.call-done.wdown_ref.wq_ref.wk_ref.wv_ref, f32[1,1024]{1,0:T(1,128)} %bitcast.244), custom_call_target="tpu_custom_call" | custom-call | flops 8589934592 | bytes 26000000 | tf_op jit(solution)/shard_map/finish/pallas_call | solution.py:341
  (282 shorter events, 201.8 us)
Async XLA Ops:
  7.2 92.9 %all-gather.7.cloned.1.call-start = ((), (), s32[]{:S(2)}) async-start(), calls=%async_computation.5 | async-start | bytes 18874368 | tf_op jit(solution)/shard_map/all_gather | solution.py:447
  12.7 173.4 %all-gather.9.cloned.1.call-start = ((), (), s32[]{:S(2)}) async-start(), calls=%async_computation.6 | async-start | bytes 18874368 | tf_op jit(solution)/shard_map/all_gather | solution.py:447
  25.1 247.6 %all-gather.11.cloned.1.call-start = ((), (), s32[]{:S(2)}) async-start(), calls=%async_computation.7 | async-start | bytes 18874368 | tf_op jit(solution)/shard_map/all_gather | solution.py:447
  25.8 694.5 %reduce-scatter.14.cloned.1.call-start = ((), (), s32[]{:S(2)}) async-start(), calls=%async_computation.12 | async-start | bytes 10485760 | tf_op jit(solution)/shard_map/reduce_scatter | solution.py:450
  229.1 18.4 %collective-permute-start.4 = (bf16[1024,4096]{1,0:T(8,128)(2,1)}, bf16[1024,4096]{1,0:T(8,128)(2,1)}, u32[]{:S(2)}, u32[]{:S(2)}) collective-permute-start(bf16[1024,4096]{1,0:T(8,128)(2,1)} %get-tuple-element.121.lhs_ref.act_ref), channel_id=1, source_target_pairs={{0,1},{1,0},{2,3},{3,2},{4,5},{5,4},{6,7},{7,6}} | collective-permute-start | bytes 25165832 | tf_op jit(solution)/shard_map/ppermute | solution.py:441
  229.5 18.0 %collective-permute-start.5 = (bf16[1024,1024]{1,0:T(8,128)(2,1)}, bf16[1024,1024]{1,0:T(8,128)(2,1)}, u32[]{:S(2)}, u32[]{:S(2)}) collective-permute-start(bf16[1024,1024]{1,0:T(8,128)(2,1)} %bitcast.25.rhs_ref.grad_ref.refs_19_), channel_id=1, source_target_pairs={{0,1},{1,0},{2,3},{3,2},{4,5},{5,4},{6,7},{7,6}} | collective-permute-start | bytes 6291464 | tf_op jit(solution)/shard_map/ppermute | solution.py:441
  262.8 561.5 %reduce-scatter.12.cloned.1.call-start = ((), (), s32[]{:S(2)}) async-start(), calls=%async_computation.11 | async-start | bytes 10485760 | tf_op jit(solution)/shard_map/reduce_scatter | solution.py:450
  295.2 47.0 %collective-permute-start.7 = (bf16[1024,4096]{1,0:T(8,128)(2,1)}, bf16[1024,4096]{1,0:T(8,128)(2,1)}, u32[]{:S(2)}, u32[]{:S(2)}) collective-permute-start(bf16[1024,4096]{1,0:T(8,128)(2,1)} %get-tuple-element.104.refs_9_), channel_id=1, source_target_pairs={{0,1},{1,0},{2,3},{3,2},{4,5},{5,4},{6,7},{7,6}} | collective-permute-start | bytes 25165832 | tf_op jit(solution)/shard_map/ppermute | solution.py:441
  295.4 46.8 %collective-permute-start.3 = (bf16[1024,1024]{1,0:T(8,128)(2,1)S(1)}, bf16[1024,1024]{1,0:T(8,128)(2,1)}, u32[]{:S(2)}, u32[]{:S(2)}) collective-permute-start(bf16[1024,1024]{1,0:T(8,128)(2,1)S(1)} %fusion.37.h_ref.refs_1_.refs_2_.refs_3_.refs_4_), channel_id=1, source_target_pairs={{0,1},{1,0},{2,3},{3,2},{4,5},{5,4},{6,7},{7,6}} | collective-permute-start | bytes 6291464 | tf_op jit(solution)/shard_map/ppermute | solution.py:441
  358.7 465.5 %reduce-scatter.10.cloned.1.call-start = ((), (), s32[]{:S(2)}) async-start(), calls=%async_computation.10 | async-start | bytes 10485760 | tf_op jit(solution)/shard_map/reduce_scatter | solution.py:450
  413.1 14.7 %collective-permute-start.8 = (bf16[3,1024,1024]{2,1,0:T(8,128)(2,1)}, bf16[3,1024,1024]{2,1,0:T(8,128)(2,1)}, u32[]{:S(2)}, u32[]{:S(2)}) collective-permute-start(bf16[3,1024,1024]{2,1,0:T(8,128)(2,1)} %get-tuple-element.103.refs_17_), channel_id=1, source_target_pairs={{0,1},{1,0},{2,3},{3,2},{4,5},{5,4},{6,7},{7,6}} | collective-permute-start | bytes 18874376 | tf_op jit(solution)/shard_map/ppermute | solution.py:441
  413.1 13.3 %collective-permute-start.6 = (bf16[1024,1024]{1,0:T(8,128)(2,1)S(1)}, bf16[1024,1024]{1,0:T(8,128)(2,1)S(1)}, u32[]{:S(2)}, u32[]{:S(2)}) collective-permute-start(bf16[1024,1024]{1,0:T(8,128)(2,1)S(1)} %copy-done.5), channel_id=1, source_target_pairs={{0,1},{1,0},{2,3},{3,2},{4,5},{5,4},{6,7},{7,6}} | collective-permute-start | bytes 6291464 | tf_op jit(solution)/shard_map/ppermute | solution.py:441
  446.5 384.5 %reduce-scatter.8.cloned.1.call-start = ((), (), s32[]{:S(2)}) async-start(), calls=%async_computation.9 | async-start | bytes 10485760 | tf_op jit(solution)/shard_map/reduce_scatter | solution.py:450
  446.6 51.3 %collective-permute-start.2 = (bf16[1024,4096]{1,0:T(8,128)(2,1)}, bf16[1024,4096]{1,0:T(8,128)(2,1)}, u32[]{:S(2)}, u32[]{:S(2)}) collective-permute-start(bf16[1024,4096]{1,0:T(8,128)(2,1)} %get-tuple-element.88.act_ref.lhs_ref), channel_id=1, source_target_pairs={{0,1},{1,0},{2,3},{3,2},{4,5},{5,4},{6,7},{7,6}} | collective-permute-start | bytes 25165832 | tf_op jit(solution)/shard_map/ppermute | solution.py:441
  496.9 47.7 %collective-permute-start.12 = (bf16[1024,4096]{1,0:T(8,128)(2,1)}, bf16[1024,4096]{1,0:T(8,128)(2,1)}, u32[]{:S(2)}, u32[]{:S(2)}) collective-permute-start(bf16[1024,4096]{1,0:T(8,128)(2,1)} %get-tuple-element.117.refs_9_), channel_id=1, source_target_pairs={{0,1},{1,0},{2,3},{3,2},{4,5},{5,4},{6,7},{7,6}} | collective-permute-start | bytes 25165832 | tf_op jit(solution)/shard_map/ppermute | solution.py:441
  497.4 16.1 %collective-permute-start.9 = (bf16[1024,1024]{1,0:T(8,128)(2,1)}, bf16[1024,1024]{1,0:T(8,128)(2,1)}, u32[]{:S(2)}, u32[]{:S(2)}) collective-permute-start(bf16[1024,1024]{1,0:T(8,128)(2,1)} %get-tuple-element.112.grad_ref.rhs_ref.refs_19_), channel_id=1, source_target_pairs={{0,1},{1,0},{2,3},{3,2},{4,5},{5,4},{6,7},{7,6}} | collective-permute-start | bytes 6291464 | tf_op jit(solution)/shard_map/ppermute | solution.py:441
  497.4 47.2 %collective-permute-start = (bf16[1024,1024]{1,0:T(8,128)(2,1)S(1)}, bf16[1024,1024]{1,0:T(8,128)(2,1)}, u32[]{:S(2)}, u32[]{:S(2)}) collective-permute-start(bf16[1024,1024]{1,0:T(8,128)(2,1)S(1)} %copy-done.1), channel_id=1, source_target_pairs={{0,1},{1,0},{2,3},{3,2},{4,5},{5,4},{6,7},{7,6}} | collective-permute-start | bytes 6291464 | tf_op jit(solution)/shard_map/ppermute | solution.py:441
  561.3 269.7 %reduce-scatter.6.cloned.1.call-start = ((), (), s32[]{:S(2)}) async-start(), calls=%async_computation.8 | async-start | bytes 10485760 | tf_op jit(solution)/shard_map/reduce_scatter | solution.py:450
  609.2 90.5 %collective-permute-start.13 = (bf16[3,1024,1024]{2,1,0:T(8,128)(2,1)}, bf16[3,1024,1024]{2,1,0:T(8,128)(2,1)}, u32[]{:S(2)}, u32[]{:S(2)}) collective-permute-start(bf16[3,1024,1024]{2,1,0:T(8,128)(2,1)} %get-tuple-element.127.refs_17_), channel_id=1, source_target_pairs={{0,1},{1,0},{2,3},{3,2},{4,5},{5,4},{6,7},{7,6}} | collective-permute-start | bytes 18874376 | tf_op jit(solution)/shard_map/ppermute | solution.py:441
  611.8 70.2 %collective-permute-start.10 = (f32[2,256,1024]{2,1,0:T(8,128)S(1)}, f32[2,256,1024]{2,1,0:T(8,128)}, u32[]{:S(2)}, u32[]{:S(2)}) collective-permute-start(f32[2,256,1024]{2,1,0:T(8,128)S(1)} %dynamic-slice_bitcast_fusion.1), channel_id=1, source_target_pairs={{0,2},{1,3},{2,0},{3,1},{4,6},{5,7},{6,4},{7,5}} | collective-permute-start | bytes 6291464 | tf_op jit(solution)/shard_map/ppermute | solution.py:444
  613.2 70.0 %collective-permute-start.11 = (f32[2,256,1024]{2,1,0:T(8,128)S(1)}, f32[2,256,1024]{2,1,0:T(8,128)}, u32[]{:S(2)}, u32[]{:S(2)}) collective-permute-start(f32[2,256,1024]{2,1,0:T(8,128)S(1)} %dynamic-slice_bitcast_fusion), channel_id=1, source_target_pairs={{0,4},{1,5},{2,6},{3,7},{4,0},{5,1},{6,2},{7,3}} | collective-permute-start | bytes 6291464 | tf_op jit(solution)/shard_map/ppermute | solution.py:444
  613.6 84.8 %collective-permute-start.1 = (bf16[1024,1024]{1,0:T(8,128)(2,1)S(1)}, bf16[1024,1024]{1,0:T(8,128)(2,1)S(1)}, u32[]{:S(2)}, u32[]{:S(2)}) collective-permute-start(bf16[1024,1024]{1,0:T(8,128)(2,1)S(1)} %copy-done.7), channel_id=1, source_target_pairs={{0,1},{1,0},{2,3},{3,2},{4,5},{5,4},{6,7},{7,6}} | collective-permute-start | bytes 6291464 | tf_op jit(solution)/shard_map/ppermute | solution.py:441
  727.0 48.1 %collective-permute-start.14 = (f32[256,1024]{1,0:T(8,128)}, f32[256,1024]{1,0:T(8,128)S(1)}, u32[]{:S(2)}, u32[]{:S(2)}) collective-permute-start(f32[256,1024]{1,0:T(8,128)} %get-tuple-element.171), channel_id=1, source_target_pairs={{0,4},{1,5},{2,6},{3,7},{4,0},{5,1},{6,2},{7,3}} | collective-permute-start | bytes 3145736 | tf_op jit(solution)/shard_map/ppermute | solution.py:444
  731.5 48.1 %collective-permute-start.15 = (f32[256,1024]{1,0:T(8,128)}, f32[256,1024]{1,0:T(8,128)S(1)}, u32[]{:S(2)}, u32[]{:S(2)}) collective-permute-start(f32[256,1024]{1,0:T(8,128)} %get-tuple-element.169), channel_id=1, source_target_pairs={{0,2},{1,3},{2,0},{3,1},{4,6},{5,7},{6,4},{7,5}} | collective-permute-start | bytes 3145736 | tf_op jit(solution)/shard_map/ppermute | solution.py:444
  (55 other events, 814.8 us)
Sparse Core Ops, SparseCore 0:
  12.8 87.1 all-gather.6
  101.9 84.1 all-gather.8
  188.5 84.1 all-gather.10
  275.5 80.7 reduce-scatter.13
  359.2 80.7 reduce-scatter.11
  446.6 80.4 reduce-scatter.9
  561.4 103.2 reduce-scatter.7
  718.4 106.0 reduce-scatter.5
where the time goes:
time: 853 us; the launch traced here: 846 us
  Pallas kernels  386 us (45%)
  waiting for transfers between devices  205 us (24%)
  matrix products  126 us (15%)
  local copies, waits for them, and re-layouts  41.7 us (5%)
  other arithmetic  34.1 us (4%)
  blocking collectives  30.2 us (4%)
  between operations  15.8 us (2%)
    ppermute x4, waiting for transfers between devices, hop(): lax.ppermute(values, AXIS_NAME, [(i, i ^ offset) for i in range(group_siz...  97.7 us
    pallas_call x2, Pallas kernels, attn_bwd(): pl.pallas_call(attn_bwd_kernel, grid=(STEPS,), in_specs=[wide, pl.BlockSp...  96.1 us
    pallas_call x2, Pallas kernels, attn_fwd(): pl.pallas_call(attn_fwd_kernel, grid=(STEPS,), in_specs=[full] + w_specs...  93.1 us
    dot_general x10, matrix products, nt(): lax.dot_general(a, b, (((1,), (1,)), ((), ())), preferred_element_type=F32)  73.4 us
    all_gather x3, waiting for transfers between devices, gather(): return lax.all_gather(values, AXIS_NAME, axis=0, tiled=True)  71.6 us
    pallas_call x4, Pallas kernels, wgrad_cols(): pl.pallas_call(functools.partial(wgrad_cols_kernel, tuple(plan)), grid_sp...  70.3 us
    dot_general x4, matrix products, nn(): lax.dot_general(a, b, (((1,), (0,)), ((), ())), preferred_element_type=F32)  53 us
    pallas_call x2, Pallas kernels, mlp_pull(): pl.pallas_call(mlp_pull_kernel, grid=(FF // TILE,), in_specs=[full, pl.Bl...  44.4 us
  transfers between devices with their start and end apart: 24, of which 10 were waited for; matrix products, arithmetic and copies ran while one was open for 23% of the time, Pallas kernels for 44%

commit v1 on v0

--- a/solution.py
+++ b/solution.py
@@ -499,9 +499,11 @@
             send_first, send_second = pick(first, 1 - along_x, 1), pick(second, 1 - along_y, 0)
             got_first = hop(send_first, 2)
             got_second = hop(send_second, 4)
-            return first, second, got_first, got_second
-
-        def ring_turn(first, second, got_first, got_second):
+            return dw, got_first, got_second
+
+        def ring_turn(dw, got_first, got_second):
+            parts = dw.reshape(2, 2, 2, dw.shape[0] // 8, dw.shape[1])
+            first, second = parts[:, :, 0], parts[:, :, 1]
             sum_first = pick(first, along_x, 1) + got_first
             sum_second = pick(second, along_y, 0) + got_second
             kept = pick(sum_first, along_y, 0), pick(sum_second, along_x, 0)
@@ -556,13 +558,12 @@
         little1 = pack(g_gain, g_lbias, g_bias1, top, g_bup1)
 
         midx = exchange(mid)
+        mid, midx = bar(mid, midx)
         pre0, g_bup0 = mlp_pull(mid, (second, 1), up_pre0)
         pre0x = exchange(pre0)
         pre0_a, mid_a = bar(pre0, mid)
         sent = ring_send(wgrad_rows(core_arr, act0, act0x, mid_a, midx))
-        first, second_half, got_first, got_second = sent
-        first, second_half, mid_b, pre0_b = bar(first, second_half, mid_a, pre0_a)
-        sent = (first, second_half, got_first, got_second)
+        mid_b, pre0_b = mid_a, pre0_a
         go0 = nt(mid_b, wide0[:, out_cols]).astype(BF16)
         dw = wgrad_cols(core_arr, [(h0, h0x)], [(0, pre0_b, pre0x)])
         dw, go0 = bar(dw, go0)

time: 853 us -> 826 us (0.968)
  waiting for transfers between devices: 205 us -> 158 us
  blocking collectives: 30.2 us -> 55.1 us
    ppermute x4, waiting for transfers between devices: 97.7 us -> 52.9 us  [hop(): lax.ppermute(values, AXIS_NAME, [(i, i ^ offset) for i in range(group_siz...]
    all_gather x2, blocking collectives: 30.2 us -> 55.1 us  [gather(): return lax.all_gather(values, AXIS_NAME, axis=0, tiled=True)]
  transfers between devices with their start and end apart: 24 -> 24, of which waited for: 10 -> 8; matrix products, arithmetic and copies ran while one was open for 23% -> 23% of each run, Pallas kernels for 44% -> 46%
where the time goes in v1:
time: 826 us; the launch traced here: 819 us
  Pallas kernels  387 us (47%)
  waiting for transfers between devices  158 us (19%)
  matrix products  126 us (15%)
  blocking collectives  55.1 us (7%)
  local copies, waits for them, and re-layouts  40.2 us (5%)
  other arithmetic  29.4 us (4%)
  between operations  15.9 us (2%)
    pallas_call x2, Pallas kernels, attn_bwd(): pl.pallas_call(attn_bwd_kernel, grid=(STEPS,), in_specs=[wide, pl.BlockSp...  96.1 us
    pallas_call x2, Pallas kernels, attn_fwd(): pl.pallas_call(attn_fwd_kernel, grid=(STEPS,), in_specs=[full] + w_specs...  93.1 us
    dot_general x10, matrix products, nt(): lax.dot_general(a, b, (((1,), (1,)), ((), ())), preferred_element_type=F32)  72.7 us
    all_gather x3, waiting for transfers between devices, gather(): return lax.all_gather(values, AXIS_NAME, axis=0, tiled=True)  71.7 us
    pallas_call x4, Pallas kernels, wgrad_cols(): pl.pallas_call(functools.partial(wgrad_cols_kernel, tuple(plan)), grid_sp...  70.2 us
    all_gather x2, blocking collectives, gather(): return lax.all_gather(values, AXIS_NAME, axis=0, tiled=True)  55.1 us
    dot_general x4, matrix products, nn(): lax.dot_general(a, b, (((1,), (0,)), ((), ())), preferred_element_type=F32)  53 us
    ppermute x4, waiting for transfers between devices, hop(): lax.ppermute(values, AXIS_NAME, [(i, i ^ offset) for i in range(group_siz...  52.9 us
  transfers between devices with their start and end apart: 24, of which 8 were waited for; matrix products, arithmetic and copies ran while one was open for 23% of the time, Pallas kernels for 46%

profile of v1, /device:TPU:0, one launch (start us, length us, event | category | flops | bytes accessed | tf_op | source)
XLA Modules:
  0.0 818.9 jit_solution(18094301276126820826)
XLA Ops:
  26.2 14.5 %all-gather.2 = bf16[8,2,1408]{2,1,0:T(2,128)(2,1)S(1)} all-gather(bf16[1,2,1408]{2,1,0:T(2,128)(2,1)S(1)} %bitcast.242), channel_id=2, replica_groups=mesh['fsdp'=8] {'fsdp'}, dimensions={0}, use_global_device_ids=true | all-gather | bytes 50688 | tf_op jit(solution)/shard_map/all_gather | solution.py:447
  51.8 48.2 %all-gather.7.cloned.1.call-done.wq_ref.wk_ref.wv_ref = bf16[1024,8192]{1,0:T(8,128)(2,1)} async-done(((bf16[128,8192]{1,0:T(8,128)(2,1)}), bf16[1024,8192]{1,0:T(8,128)(2,1)}) %all-gather.7.cloned.1.call-update) | async-done | bytes 16777232 | tf_op jit(solution)/shard_map/all_gather | solution.py:447
  100.1 46.6 %attn_fwd.2 = (bf16[3,1024,1024]{2,1,0:T(8,128)(2,1)}, bf16[1024,1024]{1,0:T(8,128)(2,1)}, f32[4,8,1024]{2,1,0:T(8,128)}) custom-call(bf16[1024,1024]{1,0:T(8,128)(2,1)} %fusion.44.h_ref.refs_1_.refs_2_.refs_3_.refs_4_, bf16[1024,8192]{1,0:T(8,128)(2,1)} %all-gather.7.cloned.1.call-done.wq_ref.wk_ref.wv_ref, ...), custom_call_target="tpu_custom_call" | custom-call | flops 20000000000 | bytes 20000000 | tf_op jit(solution)/shard_map/attn_fwd/pallas_call | solution.py:109
  153.5 19.1 %fusion.7 = (bf16[1024,4096]{1,0:T(8,128)(2,1)}, f32[1024,4096]{1,0:T(8,128)}) fusion(f32[4096]{0:T(1024)S(1)} %bitcast.235, bf16[1024,1024]{1,0:T(8,128)(2,1)S(1)} %copy-done, bf16[1024,8192]{1,0:T(8,128)(2,1)} %all-gather.7.cloned.1.call-done.wq_ref.wk_ref.wv_ref), kind=kOutput, calls=%fused_computation.9 | convolution fusion | flops 8631877632 | bytes 35667968 | tf_op jit(solution)/shard_map/dot_general | solution.py:56
  172.5 13.5 %all-gather.9.cloned.1.call-done.wdown_ref = bf16[1024,8192]{1,0:T(8,128)(2,1)} async-done(((bf16[128,8192]{1,0:T(8,128)(2,1)}), bf16[1024,8192]{1,0:T(8,128)(2,1)}) %all-gather.9.cloned.1.call-update) | async-done | bytes 16777232 | tf_op jit(solution)/shard_map/all_gather | solution.py:447
  186.1 16.5 %finish.2 = bf16[1024,1024]{1,0:T(8,128)(2,1)} custom-call(f32[1024,1024]{1,0:T(8,128)} %fusion.50.base_ref, bf16[1024,4096]{1,0:T(8,128)(2,1)} %get-tuple-element.85.act_ref.lhs_ref, bf16[1024,8192]{1,0:T(8,128)(2,1)} %all-gather.9.cloned.1.call-done.wdown_ref, f32[1,1024]{1,0:T(1,128)} %bitcast.247), custom_call_target="tpu_custom_call" | custom-call | flops 8589934592 | bytes 26000000 | tf_op jit(solution)/shard_map/finish/pallas_call | solution.py:341
  207.8 21.2 %fusion.15 = (bf16[1024,4096]{1,0:T(8,128)(2,1)}, f32[1024,4096]{1,0:T(8,128)}) fusion(f32[4096]{0:T(1024)S(1)} %bitcast.234, bf16[1024,1024]{1,0:T(8,128)(2,1)S(1)} %fusion.37.h_ref.refs_1_.refs_2_.refs_3_.refs_4_, bf16[1024,8192]{1,0:T(8,128)(2,1)} %all-gather.9.cloned.1.call-done.wdown_ref), kind=kOutput, calls=%fused_computation.17 | convolution fusion | flops 8631877632 | bytes 35667968 | tf_op jit(solution)/shard_map/dot_general | solution.py:56
  229.6 17.9 %collective-permute-done.5.rhs2_ref.refs_20_ = bf16[1024,1024]{1,0:T(8,128)(2,1)} collective-permute-done((bf16[1024,1024]{1,0:T(8,128)(2,1)}, bf16[1024,1024]{1,0:T(8,128)(2,1)}, u32[]{:S(2)}, u32[]{:S(2)}) %collective-permute-start.5) | collective-permute-done | bytes 2097184 | tf_op jit(solution)/shard_map/ppermute | solution.py:441
  247.5 15.2 %wgrad_rows.2 = f32[2048,1024]{1,0:T(8,128)} custom-call(s32[1]{0:T(128)} %bitcast.24.core_ref.refs_0_, bf16[1024,4096]{1,0:T(8,128)(2,1)} %get-tuple-element.116.lhs_ref.act_ref, bf16[1024,4096]{1,0:T(8,128)(2,1)} %collective-permute-done.4.lhs2_ref, bf16[1024,1024]{1,0:T(8,128)(2,1)} %bitcast.25.rhs_ref.grad_ref.refs_19_, ...), custom_call_target="tpu_custom_call" | custom-call | flops 8589934592 | bytes 20000000 | tf_op jit(solution)/shard_map/wgrad_rows/pallas_call | solution.py:191
  272.7 22.5 %mlp_pull.2 = (bf16[1024,4096]{1,0:T(8,128)(2,1)}, f32[8,4096]{1,0:T(8,128)}) custom-call(bf16[1024,1024]{1,0:T(8,128)(2,1)} %bitcast.25.rhs_ref.grad_ref.refs_19_, bf16[1024,8192]{1,0:T(8,128)(2,1)} %all-gather.11.cloned.1.call-done.wdown_ref.wq_ref.wk_ref.wv_ref, f32[1024,4096]{1,0:T(8,128)} %get-tuple-element.212.pre_ref), custom_call_target="tpu_custom_call" | custom-call | flops 8589934592 | bytes 36000000 | tf_op jit(solution)/shard_map/mlp_pull/pallas_call | solution.py:374
  295.7 46.5 %attn_fwd.3 = (bf16[3,1024,1024]{2,1,0:T(8,128)(2,1)}, bf16[1024,1024]{1,0:T(8,128)(2,1)}, f32[4,8,1024]{2,1,0:T(8,128)}) custom-call(bf16[1024,1024]{1,0:T(8,128)(2,1)} %copy-done.2, bf16[1024,8192]{1,0:T(8,128)(2,1)} %all-gather.11.cloned.1.call-done.wdown_ref.wq_ref.wk_ref.wv_ref, ...), custom_call_target="tpu_custom_call" | custom-call | flops 20000000000 | bytes 20000000 | tf_op jit(solution)/shard_map/attn_fwd/pallas_call | solution.py:109
  342.2 16.5 %wgrad_cols.4 = f32[512,4096]{1,0:T(8,128)} custom-call(s32[1]{0:T(128)} %bitcast.24.core_ref.refs_0_, bf16[1024,1024]{1,0:T(8,128)(2,1)} %copy-done.2, bf16[1024,1024]{1,0:T(8,128)(2,1)} %copy-done.2, bf16[1024,1024]{1,0:T(8,128)(2,1)} %copy-done.2, bf16[1024,1024]{1,0:T(8,128)(2,1)} %copy-done.2, ...), custom_call_target="tpu_custom_call" | custom-call | flops 8589934592 | bytes 25600000 | tf_op jit(solution)/shard_map/wgrad_cols/pallas_call | solution.py:258
  364.9 48.1 %attn_bwd.2 = (bf16[3,1024,1024]{2,1,0:T(8,128)(2,1)}, f32[8,3072]{1,0:T(8,128)}) custom-call(bf16[3,1024,1024]{2,1,0:T(8,128)(2,1)} %get-tuple-element.92.qkv_ref, bf16[1024,1024]{1,0:T(8,128)(2,1)} %convolution_convert_fusion.1.go_ref, f32[4,8,1024]{2,1,0:T(8,128)} %get-tuple-element.95.lse_ref, f32[1024,256]{1,0:T(8,128)} %copy.106.keep_ref, ...), custom_call_target="tpu_custom_call" | custom-call | flops 49999998976 | bytes 20000000 | tf_op jit(solution)/shard_map/attn_bwd/pallas_call | solution.py:170
  427.8 18.7 %wgrad_cols.5 = f32[512,4096]{1,0:T(8,128)} custom-call(s32[1]{0:T(128)} %bitcast.24.core_ref.refs_0_, bf16[1024,1024]{1,0:T(8,128)(2,1)} %copy-done.2, bf16[1024,1024]{1,0:T(8,128)(2,1)} %copy-done.2, bf16[1024,1024]{1,0:T(8,128)(2,1)} %copy-done.2, bf16[1024,1024]{1,0:T(8,128)(2,1)} %copy-done.2, ...), custom_call_target="tpu_custom_call" | custom-call | flops 8589934592 | bytes 25600000 | tf_op jit(solution)/shard_map/wgrad_cols/pallas_call | solution.py:258
  453.4 16.3 %fusion.41 = (f32[1024]{0:T(1024)S(1)}, f32[1024]{0:T(1024)S(1)}, f32[1024]{0:T(1024)S(1)}, f32[1024]{0:T(1024)S(1)}, f32[1024,1024]{1,0:T(8,128)S(1)}) fusion(bf16[1024,1024]{1,0:T(8,128)(2,1)S(1)} %copy-done.12, f32[1024]{0:T(1024)S(1)} %copy-done.38, f32[1024]{0:T(1024)S(1)} %copy-done.34, f32[1024]{0:T(1024)S(1)} %copy-done.40, ...), kind=kOutput, calls=%fused_computation.54 | convolution fusion | flops 8602513408 | bytes 31485952 | tf_op jit(solution)/shard_map/dot_general | solution.py:52
  478.6 21.8 %mlp_pull.3 = (bf16[1024,4096]{1,0:T(8,128)(2,1)}, f32[8,4096]{1,0:T(8,128)}) custom-call(bf16[1024,1024]{1,0:T(8,128)(2,1)} %copy-done.14, bf16[1024,8192]{1,0:T(8,128)(2,1)} %all-gather.9.cloned.1.call-done.wdown_ref, f32[1024,4096]{1,0:T(8,128)} %get-tuple-element.210.pre_ref), custom_call_target="tpu_custom_call" | custom-call | flops 8589934592 | bytes 36000000 | tf_op jit(solution)/shard_map/mlp_pull/pallas_call | solution.py:374
  518.1 16.5 %wgrad_cols.6 = f32[512,4096]{1,0:T(8,128)} custom-call(s32[1]{0:T(128)} %bitcast.24.core_ref.refs_0_, bf16[1024,1024]{1,0:T(8,128)(2,1)} %fusion.44.h_ref.refs_1_.refs_2_.refs_3_.refs_4_, bf16[1024,1024]{1,0:T(8,128)(2,1)} %fusion.44.h_ref.refs_1_.refs_2_.refs_3_.refs_4_, bf16[1024,1024]{1,0:T(8,128)(2,1)} %fusion.44.h_ref.refs_1_.refs_2_.refs_3_.refs_4_, ...), custom_call_target="tpu_custom_call" | custom-call | flops 8589934592 | bytes 25600000 | tf_op jit(solution)/shard_map/wgrad_cols/pallas_call | solution.py:258
  534.8 48.0 %attn_bwd.3 = (bf16[3,1024,1024]{2,1,0:T(8,128)(2,1)}, f32[8,3072]{1,0:T(8,128)}) custom-call(bf16[3,1024,1024]{2,1,0:T(8,128)(2,1)} %get-tuple-element.106.qkv_ref, bf16[1024,1024]{1,0:T(8,128)(2,1)} %convolution_convert_fusion.go_ref, f32[4,8,1024]{2,1,0:T(8,128)} %get-tuple-element.109.lse_ref, f32[1024,256]{1,0:T(8,128)} %copy.106.keep_ref, ...), custom_call_target="tpu_custom_call" | custom-call | flops 49999998976 | bytes 20000000 | tf_op jit(solution)/shard_map/attn_bwd/pallas_call | solution.py:170
  583.2 15.5 %wgrad_rows.3 = f32[2048,1024]{1,0:T(8,128)} custom-call(s32[1]{0:T(128)} %bitcast.24.core_ref.refs_0_, bf16[1024,4096]{1,0:T(8,128)(2,1)} %get-tuple-element.85.act_ref.lhs_ref, bf16[1024,4096]{1,0:T(8,128)(2,1)} %collective-permute-done.2.lhs2_ref, bf16[1024,1024]{1,0:T(8,128)(2,1)} %copy-done.14, bf16[1024,1024]{1,0:T(8,128)(2,1)} %copy-done.18), custom_call_target="tpu_custom_call" | custom-call | flops 8589934592 | bytes 20000000 | tf_op jit(solution)/shard_map/wgrad_rows/pallas_call | solution.py:191
  605.8 52.9 %collective-permute-done.10 = f32[2,256,1024]{2,1,0:T(8,128)S(1)} collective-permute-done((f32[2,256,1024]{2,1,0:T(8,128)S(1)}, f32[2,256,1024]{2,1,0:T(8,128)S(1)}, u32[]{:S(2)}, u32[]{:S(2)}) %collective-permute-start.10) | collective-permute-done | bytes 2097184 | tf_op jit(solution)/shard_map/ppermute | solution.py:444
  658.7 14.0 %fusion.19 = f32[1024,1024]{1,0:T(8,128)} fusion(bf16[1024,4096]{1,0:T(8,128)(2,1)S(1)} %bitcast.213, bf16[1024,8192]{1,0:T(8,128)(2,1)} %all-gather.7.cloned.1.call-done.wq_ref.wk_ref.wv_ref), kind=kOutput, calls=%fused_computation.23 | convolution fusion | flops 8589934592 | bytes 20971520 | tf_op jit(solution)/shard_map/dot_general | solution.py:52
  674.1 18.5 %wgrad_cols.7 = f32[512,4096]{1,0:T(8,128)} custom-call(s32[1]{0:T(128)} %bitcast.24.core_ref.refs_0_, bf16[1024,1024]{1,0:T(8,128)(2,1)} %fusion.44.h_ref.refs_1_.refs_2_.refs_3_.refs_4_, bf16[1024,1024]{1,0:T(8,128)(2,1)} %fusion.44.h_ref.refs_1_.refs_2_.refs_3_.refs_4_, bf16[1024,1024]{1,0:T(8,128)(2,1)} %fusion.44.h_ref.refs_1_.refs_2_.refs_3_.refs_4_, ...), custom_call_target="tpu_custom_call" | custom-call | flops 8589934592 | bytes 25600000 | tf_op jit(solution)/shard_map/wgrad_cols/pallas_call | solution.py:258
  725.7 40.6 %all-gather.1 = f32[64,2,1280]{2,0,1:T(8,128)S(1)} all-gather(f32[8,2,1280]{2,0,1:T(8,128)S(1)} %pad_maximum_fusion.1), channel_id=3, replica_groups=mesh['fsdp'=8] {'fsdp'}, dimensions={0}, use_global_device_ids=true | all-gather | bytes 737280 | tf_op jit(solution)/shard_map/all_gather | solution.py:447
  788.0 16.2 %finish.3 = bf16[1024,1024]{1,0:T(8,128)(2,1)} custom-call(f32[1024,1024]{1,0:T(8,128)} %fusion.53.base_ref, bf16[1024,4096]{1,0:T(8,128)(2,1)} %get-tuple-element.116.lhs_ref.act_ref, bf16[1024,8192]{1,0:T(8,128)(2,1)} %all-gather.11.cloned.1.call-done.wdown_ref.wq_ref.wk_ref.wv_ref, f32[1,1024]{1,0:T(1,128)} %bitcast.243), custom_call_target="tpu_custom_call" | custom-call | flops 8589934592 | bytes 26000000 | tf_op jit(solution)/shard_map/finish/pallas_call | solution.py:341
  (292 shorter events, 177.5 us)
Async XLA Ops:
  7.2 92.9 %all-gather.7.cloned.1.call-start = ((), (), s32[]{:S(2)}) async-start(), calls=%async_computation.5 | async-start | bytes 18874368 | tf_op jit(solution)/shard_map/all_gather | solution.py:447
  12.7 173.4 %all-gather.9.cloned.1.call-start = ((), (), s32[]{:S(2)}) async-start(), calls=%async_computation.6 | async-start | bytes 18874368 | tf_op jit(solution)/shard_map/all_gather | solution.py:447
  25.1 247.6 %all-gather.11.cloned.1.call-start = ((), (), s32[]{:S(2)}) async-start(), calls=%async_computation.7 | async-start | bytes 18874368 | tf_op jit(solution)/shard_map/all_gather | solution.py:447
  25.8 668.8 %reduce-scatter.14.cloned.1.call-start = ((), (), s32[]{:S(2)}) async-start(), calls=%async_computation.12 | async-start | bytes 10485760 | tf_op jit(solution)/shard_map/reduce_scatter | solution.py:450
  229.1 18.4 %collective-permute-start.4 = (bf16[1024,4096]{1,0:T(8,128)(2,1)}, bf16[1024,4096]{1,0:T(8,128)(2,1)}, u32[]{:S(2)}, u32[]{:S(2)}) collective-permute-start(bf16[1024,4096]{1,0:T(8,128)(2,1)} %get-tuple-element.116.lhs_ref.act_ref), channel_id=1, source_target_pairs={{0,1},{1,0},{2,3},{3,2},{4,5},{5,4},{6,7},{7,6}} | collective-permute-start | bytes 25165832 | tf_op jit(solution)/shard_map/ppermute | solution.py:441
  229.5 18.0 %collective-permute-start.5 = (bf16[1024,1024]{1,0:T(8,128)(2,1)}, bf16[1024,1024]{1,0:T(8,128)(2,1)}, u32[]{:S(2)}, u32[]{:S(2)}) collective-permute-start(bf16[1024,1024]{1,0:T(8,128)(2,1)} %bitcast.25.rhs_ref.grad_ref.refs_19_), channel_id=1, source_target_pairs={{0,1},{1,0},{2,3},{3,2},{4,5},{5,4},{6,7},{7,6}} | collective-permute-start | bytes 6291464 | tf_op jit(solution)/shard_map/ppermute | solution.py:441
  262.7 504.9 %reduce-scatter.12.cloned.1.call-start = ((), (), s32[]{:S(2)}) async-start(), calls=%async_computation.11 | async-start | bytes 10485760 | tf_op jit(solution)/shard_map/reduce_scatter | solution.py:450
  295.2 47.0 %collective-permute-start.7 = (bf16[1024,4096]{1,0:T(8,128)(2,1)}, bf16[1024,4096]{1,0:T(8,128)(2,1)}, u32[]{:S(2)}, u32[]{:S(2)}) collective-permute-start(bf16[1024,4096]{1,0:T(8,128)(2,1)} %get-tuple-element.101.refs_9_), channel_id=1, source_target_pairs={{0,1},{1,0},{2,3},{3,2},{4,5},{5,4},{6,7},{7,6}} | collective-permute-start | bytes 25165832 | tf_op jit(solution)/shard_map/ppermute | solution.py:441
  295.4 46.8 %collective-permute-start.3 = (bf16[1024,1024]{1,0:T(8,128)(2,1)S(1)}, bf16[1024,1024]{1,0:T(8,128)(2,1)}, u32[]{:S(2)}, u32[]{:S(2)}) collective-permute-start(bf16[1024,1024]{1,0:T(8,128)(2,1)S(1)} %fusion.37.h_ref.refs_1_.refs_2_.refs_3_.refs_4_), channel_id=1, source_target_pairs={{0,1},{1,0},{2,3},{3,2},{4,5},{5,4},{6,7},{7,6}} | collective-permute-start | bytes 6291464 | tf_op jit(solution)/shard_map/ppermute | solution.py:441
  358.8 408.9 %reduce-scatter.10.cloned.1.call-start = ((), (), s32[]{:S(2)}) async-start(), calls=%async_computation.10 | async-start | bytes 10485760 | tf_op jit(solution)/shard_map/reduce_scatter | solution.py:450
  413.1 14.7 %collective-permute-start.8 = (bf16[3,1024,1024]{2,1,0:T(8,128)(2,1)}, bf16[3,1024,1024]{2,1,0:T(8,128)(2,1)}, u32[]{:S(2)}, u32[]{:S(2)}) collective-permute-start(bf16[3,1024,1024]{2,1,0:T(8,128)(2,1)} %get-tuple-element.100.refs_17_), channel_id=1, source_target_pairs={{0,1},{1,0},{2,3},{3,2},{4,5},{5,4},{6,7},{7,6}} | collective-permute-start | bytes 18874376 | tf_op jit(solution)/shard_map/ppermute | solution.py:441
  413.2 13.3 %collective-permute-start.6 = (bf16[1024,1024]{1,0:T(8,128)(2,1)S(1)}, bf16[1024,1024]{1,0:T(8,128)(2,1)S(1)}, u32[]{:S(2)}, u32[]{:S(2)}) collective-permute-start(bf16[1024,1024]{1,0:T(8,128)(2,1)S(1)} %copy-done.6), channel_id=1, source_target_pairs={{0,1},{1,0},{2,3},{3,2},{4,5},{5,4},{6,7},{7,6}} | collective-permute-start | bytes 6291464 | tf_op jit(solution)/shard_map/ppermute | solution.py:441
  446.5 357.6 %reduce-scatter.8.cloned.1.call-start = ((), (), s32[]{:S(2)}) async-start(), calls=%async_computation.9 | async-start | bytes 10485760 | tf_op jit(solution)/shard_map/reduce_scatter | solution.py:450
  473.1 4.2 collective-permute-start.9
  500.4 17.7 %collective-permute-start.12 = (bf16[1024,4096]{1,0:T(8,128)(2,1)}, bf16[1024,4096]{1,0:T(8,128)(2,1)}, u32[]{:S(2)}, u32[]{:S(2)}) collective-permute-start(bf16[1024,4096]{1,0:T(8,128)(2,1)} %get-tuple-element.112.refs_9_), channel_id=1, source_target_pairs={{0,1},{1,0},{2,3},{3,2},{4,5},{5,4},{6,7},{7,6}} | collective-permute-start | bytes 25165832 | tf_op jit(solution)/shard_map/ppermute | solution.py:441
  500.4 16.4 %collective-permute-start = (bf16[1024,1024]{1,0:T(8,128)(2,1)S(1)}, bf16[1024,1024]{1,0:T(8,128)(2,1)S(1)}, u32[]{:S(2)}, u32[]{:S(2)}) collective-permute-start(bf16[1024,1024]{1,0:T(8,128)(2,1)S(1)} %copy-done.1), channel_id=1, source_target_pairs={{0,1},{1,0},{2,3},{3,2},{4,5},{5,4},{6,7},{7,6}} | collective-permute-start | bytes 6291464 | tf_op jit(solution)/shard_map/ppermute | solution.py:441
  534.6 269.6 %reduce-scatter.6.cloned.1.call-start = ((), (), s32[]{:S(2)}) async-start(), calls=%async_computation.8 | async-start | bytes 10485760 | tf_op jit(solution)/shard_map/reduce_scatter | solution.py:450
  534.7 48.5 %collective-permute-start.2 = (bf16[1024,4096]{1,0:T(8,128)(2,1)}, bf16[1024,4096]{1,0:T(8,128)(2,1)}, u32[]{:S(2)}, u32[]{:S(2)}) collective-permute-start(bf16[1024,4096]{1,0:T(8,128)(2,1)} %get-tuple-element.85.act_ref.lhs_ref), channel_id=1, source_target_pairs={{0,1},{1,0},{2,3},{3,2},{4,5},{5,4},{6,7},{7,6}} | collective-permute-start | bytes 25165832 | tf_op jit(solution)/shard_map/ppermute | solution.py:441
  582.7 91.4 %collective-permute-start.13 = (bf16[3,1024,1024]{2,1,0:T(8,128)(2,1)}, bf16[3,1024,1024]{2,1,0:T(8,128)(2,1)}, u32[]{:S(2)}, u32[]{:S(2)}) collective-permute-start(bf16[3,1024,1024]{2,1,0:T(8,128)(2,1)} %get-tuple-element.121.refs_17_), channel_id=1, source_target_pairs={{0,1},{1,0},{2,3},{3,2},{4,5},{5,4},{6,7},{7,6}} | collective-permute-start | bytes 18874376 | tf_op jit(solution)/shard_map/ppermute | solution.py:441
  603.7 55.0 %collective-permute-start.10 = (f32[2,256,1024]{2,1,0:T(8,128)S(1)}, f32[2,256,1024]{2,1,0:T(8,128)S(1)}, u32[]{:S(2)}, u32[]{:S(2)}) collective-permute-start(f32[2,256,1024]{2,1,0:T(8,128)S(1)} %dynamic-slice_bitcast_fusion.1), channel_id=1, source_target_pairs={{0,2},{1,3},{2,0},{3,1},{4,6},{5,7},{6,4},{7,5}} | collective-permute-start | bytes 6291464 | tf_op jit(solution)/shard_map/ppermute | solution.py:444
  605.0 53.7 %collective-permute-start.11 = (f32[2,256,1024]{2,1,0:T(8,128)S(1)}, f32[2,256,1024]{2,1,0:T(8,128)S(1)}, u32[]{:S(2)}, u32[]{:S(2)}) collective-permute-start(f32[2,256,1024]{2,1,0:T(8,128)S(1)} %dynamic-slice_bitcast_fusion), channel_id=1, source_target_pairs={{0,4},{1,5},{2,6},{3,7},{4,0},{5,1},{6,2},{7,3}} | collective-permute-start | bytes 6291464 | tf_op jit(solution)/shard_map/ppermute | solution.py:444
  605.7 67.1 %collective-permute-start.1 = (bf16[1024,1024]{1,0:T(8,128)(2,1)S(1)}, bf16[1024,1024]{1,0:T(8,128)(2,1)S(1)}, u32[]{:S(2)}, u32[]{:S(2)}) collective-permute-start(bf16[1024,1024]{1,0:T(8,128)(2,1)S(1)} %copy-done.8), channel_id=1, source_target_pairs={{0,1},{1,0},{2,3},{3,2},{4,5},{5,4},{6,7},{7,6}} | collective-permute-start | bytes 6291464 | tf_op jit(solution)/shard_map/ppermute | solution.py:441
  702.5 65.2 %collective-permute-start.15 = (f32[256,1024]{1,0:T(8,128)S(1)}, f32[256,1024]{1,0:T(8,128)}, u32[]{:S(2)}, u32[]{:S(2)}) collective-permute-start(f32[256,1024]{1,0:T(8,128)S(1)} %get-tuple-element.164), channel_id=1, source_target_pairs={{0,2},{1,3},{2,0},{3,1},{4,6},{5,7},{6,4},{7,5}} | collective-permute-start | bytes 3145736 | tf_op jit(solution)/shard_map/ppermute | solution.py:444
  705.1 62.5 %collective-permute-start.14 = (f32[256,1024]{1,0:T(8,128)S(1)}, f32[256,1024]{1,0:T(8,128)}, u32[]{:S(2)}, u32[]{:S(2)}) collective-permute-start(f32[256,1024]{1,0:T(8,128)S(1)} %get-tuple-element.166), channel_id=1, source_target_pairs={{0,4},{1,5},{2,6},{3,7},{4,0},{5,1},{6,2},{7,3}} | collective-permute-start | bytes 3145736 | tf_op jit(solution)/shard_map/ppermute | solution.py:444
  (59 other events, 906.4 us)
Sparse Core Ops, SparseCore 0:
  12.8 87.1 all-gather.6
  101.9 84.1 all-gather.8
  188.5 84.1 all-gather.10
  275.5 80.7 reduce-scatter.13
  359.2 80.7 reduce-scatter.11
  446.6 80.4 reduce-scatter.9
  534.7 87.7 reduce-scatter.7
  692.8 107.2 reduce-scatter.5
